TPU v7x, 32 devices: a 4x4x1 block of a 4x4x8 slice. The times are simulated.
32 devices in a mesh: dp: 1 (over z), tp: 4 (over y), ep: 8 (over x, core).
Axes of the slice: x: 4, y: 4, z: 1, core: 2. Of those that a mesh axis runs over, the one named last changes fastest.
The devices are a block of a 4x4x8 slice.
Arguments:
- act_in: bfloat16 [131072, 768], P(('dp', 'ep'))
- expert_idx: int32 [131072, 1], P(('dp', 'ep'))
- gate_vals: float32 [131072, 1], P(('dp', 'ep'))
- w_in: bfloat16 [16, 768, 3072], P('ep', None, 'tp')
- w_out: bfloat16 [16, 3072, 768], P('ep', 'tp')
Outputs:
- output: bfloat16 [131072, 768], P(('dp', 'ep'))
All inputs are finite; a program needn't handle non-finite values.
Results may differ from a plain program's by a relative error of at most 0.001.
Values are sent between devices in bfloat16 or wider.
A program may use at most 768 MiB of HBM per device.

v0:
```python
import jax
import jax.numpy as jnp
from jax import lax
from jax.sharding import PartitionSpec as P, NamedSharding


def capacity_of(top_k, tokens, experts, tp_size):
    divisor = 32 * experts * tp_size
    return 8 * tp_size * ((5 * top_k * tokens + divisor - 1) // divisor)


def route_slots(idx_loc, experts):
    hit_mask = idx_loc[:, :, None] == jnp.arange(experts)[None, None, :]
    per_tok = jnp.sum(hit_mask, axis=1, dtype=jnp.int32)
    preceding = jnp.cumsum(per_tok, axis=0) - per_tok
    return jnp.sum(jnp.where(hit_mask, preceding[:, None, :], 0), axis=2)


def solution(mesh):
    tp_size = mesh.shape["tp"]
    ep_size = mesh.shape["ep"]

    def local_moe(act_loc, idx_loc, gate_loc, w_in, w_out):
        tokens, hidden = act_loc.shape
        top_k = idx_loc.shape[1]
        local_experts = w_in.shape[0]
        experts = local_experts * ep_size
        capacity = capacity_of(top_k, tokens, experts, tp_size)
        slot_width = capacity // tp_size
        slot_ids = route_slots(idx_loc, experts)
        group_of = idx_loc // local_experts
        local_of = idx_loc % local_experts
        own_slot = slot_ids - lax.axis_index("tp") * slot_width
        is_sent = (own_slot >= 0) & (own_slot < slot_width)
        n_send = experts * slot_width
        send_pos = jnp.where(is_sent, (local_of * ep_size + group_of) * slot_width + own_slot, n_send).reshape(-1)
        tok_ids = jnp.broadcast_to(jnp.arange(tokens, dtype=jnp.int32)[:, None], idx_loc.shape).reshape(-1)
        tok_table = jnp.full((n_send + 1,), tokens, jnp.int32).at[send_pos].set(tok_ids)[:n_send]
        outgoing = jnp.take(act_loc, tok_table, axis=0, mode="fill", fill_value=0).reshape(local_experts, ep_size, slot_width, hidden)
        arrived = lax.all_to_all(outgoing, "ep", 1, 1, tiled=True)
        expert_in = lax.all_gather(arrived, "tp", axis=2, tiled=True)
        pre_act = jnp.einsum("escd,edf->escf", expert_in, w_in, preferred_element_type=jnp.float32)
        hidden_act = jax.nn.gelu(pre_act, approximate=True).astype(jnp.bfloat16)
        part_out = jnp.einsum("escf,efd->escd", hidden_act, w_out, preferred_element_type=jnp.float32)
        expert_out = lax.psum_scatter(part_out, "tp", scatter_dimension=2, tiled=True).astype(jnp.bfloat16)
        returned = lax.all_to_all(expert_out, "ep", 1, 1, tiled=True)
        own_out = lax.all_gather(returned, "tp", axis=2, tiled=True).reshape(experts * capacity, hidden)
        out_pos = jnp.where(slot_ids < capacity, (local_of * ep_size + group_of) * capacity + slot_ids, experts * capacity)
        picked = jnp.take(own_out, out_pos, axis=0, mode="fill", fill_value=0)
        combined = jnp.sum(gate_loc[:, :, None] * picked, axis=1)
        return combined.astype(jnp.bfloat16)

    tok_spec = P(("dp", "ep"), None)
    return jax.shard_map(local_moe, mesh=mesh, in_specs=(tok_spec, tok_spec, tok_spec, P("ep", None, "tp"), P("ep", "tp", None)), out_specs=tok_spec, check_vma=False)
```

profile of v0, /device:TPU:97, one launch (start us, length us, event | category | flops | bytes accessed | tf_op | source)
XLA Modules:
  0.0 1795.1 jit_solution(169722231001804209)
XLA Ops:
  6.5 0.0 copy-start
  6.6 0.0 all-gather.3.cloned.1.call-start
  6.6 1.1 copy.15
  7.6 0.2 fusion.15
  7.8 0.3 reduce-window.9
  8.1 1.1 broadcast_add_fusion
  9.2 1.6 copy.16
  10.7 1.8 fusion.14
  12.5 2.8 and_reduce_fusion
  15.3 0.2 compare_select_fusion
  15.5 60.4 %scatter_custom_fusion = s32[5121]{0:T(1024)S(1)} fusion(s32[16384]{0:T(1024)S(1)} %bitcast.54, s32[16384]{0:T(1024)S(1)} %iota.13, s32[]{:T(128)} %constant.77.clone.1), kind=kCustom, calls=%fused_computation.44 | custom fusion | bytes 20488 | tf_op jit(solution)/shard_map/scatter | solution.py:38
  75.8 0.1 slice.14
  76.0 34.9 %gather_fusion = bf16[5120,768]{1,0:T(8,128)(2,1)} fusion(bf16[16384,768]{1,0:T(8,128)(2,1)} %param.5, s32[5120]{0:T(1024)S(1)} %get-tuple-element.9), kind=kCustom, calls=%fused_computation | custom fusion | bytes 15749120 | tf_op jit(solution)/shard_map/jit(_take)/gather | solution.py:39
  110.9 4.3 copy_select_fusion
  115.2 93.8 %all_to_all.10 = bf16[2,8,320,768]{3,2,0,1:T(8,128)(2,1)} all-to-all(bf16[2,8,320,768]{3,2,0,1:T(8,128)(2,1)S(1)} %copy_select_fusion), channel_id=1, replica_groups=mesh['dp'=1,'tp'=4,'ep'=8] {'ep'}, dimensions={1} | all-to-all | bytes 15728640 | tf_op jit(solution)/shard_map/all_to_all | solution.py:40
  209.0 7.1 copy.19
  216.2 0.1 all-gather.3.cloned.1.call-update
  216.2 0.2 reduce-scatter.2.cloned.1.call-start
  216.5 275.2 %all-gather.3.cloned.1.call-done = bf16[2,8,1280,768]{3,2,1,0:T(8,128)(2,1)} async-done(((bf16[2,8,320,768]{3,2,1,0:T(8,128)(2,1)}), bf16[2,8,1280,768]{3,2,1,0:T(8,128)(2,1)}) %all-gather.3.cloned.1.call-update) | async-done | bytes 31457296 | tf_op jit(solution)/shard_map/all_gather | solution.py:41
  491.7 63.4 %fusion.8 = f32[2,8,1280,768]{3,2,1,0:T(8,128)} fusion(bf16[2,8,1280,768]{3,2,1,0:T(8,128)(2,1)} %all-gather.3.cloned.1.call-done, bf16[2,768,768]{2,1,0:T(8,128)(2,1)S(1)} %copy-done, bf16[2,768,768]{2,1,0:T(8,128)(2,1)} %param.8), kind=kOutput, calls=%fused_computation.14 | convolution fusion | flops 48459939840 | bytes 99090432 | tf_op jit(solution)/shard_map/escf,efd->escd/dot_general | solution.py:44
  555.1 0.1 reduce-scatter.2.cloned.1.call-update
  555.1 0.3 all-gather.5.cloned.1.call-start
  555.4 517.5 %reduce-scatter.2.cloned.1.call-done = f32[2,8,320,768]{3,2,1,0:T(8,128)} async-done(((f32[2,8,1280,768]{3,2,1,0:T(8,128)}), f32[2,8,320,768]{3,2,1,0:T(8,128)}) %reduce-scatter.2.cloned.1.call-update) | async-done | bytes 15728656 | tf_op jit(solution)/shard_map/reduce_scatter | solution.py:45
  1073.0 9.7 convert_element_type.28
  1082.6 7.0 copy.20
  1089.7 94.3 %all_to_all.11 = bf16[2,8,320,768]{3,2,0,1:T(8,128)(2,1)} all-to-all(bf16[2,8,320,768]{3,2,0,1:T(8,128)(2,1)} %copy.20), channel_id=1, replica_groups=mesh['dp'=1,'tp'=4,'ep'=8] {'ep'}, dimensions={1} | all-to-all | bytes 15728640 | tf_op jit(solution)/shard_map/all_to_all | solution.py:46
  1183.9 0.1 all-gather.5.cloned.1.call-update
  1184.0 0.0 copy-done.2
  1184.0 272.2 %all-gather.5.cloned.1.call-done = bf16[2,8,1280,768]{3,2,0,1:T(8,128)(2,1)} async-done(((bf16[2,8,320,768]{3,2,0,1:T(8,128)(2,1)}), bf16[2,8,1280,768]{3,2,0,1:T(8,128)(2,1)}) %all-gather.5.cloned.1.call-update) | async-done | bytes 31457296 | tf_op jit(solution)/shard_map/all_gather | solution.py:47
  1456.2 21.6 %copy.21 = bf16[2,8,1280,768]{3,2,1,0:T(8,128)(2,1)} copy(bf16[2,8,1280,768]{3,2,0,1:T(8,128)(2,1)} %all-gather.5.cloned.1.call-done) | data formatting | bytes 62914560 | tf_op jit(solution)/shard_map/all_gather | solution.py:47
  1477.9 285.9 %gather_fusion.1 = bf16[16384,768]{1,0:T(8,128)(2,1)} fusion(bf16[20480,768]{1,0:T(8,128)(2,1)} %bitcast.45, s32[16384]{0:T(1024)S(1)} %broadcast_clamp_fusion), kind=kCustom, calls=%fused_computation.1 | custom fusion | bytes 50397184 | tf_op jit(solution)/shard_map/jit(_take)/gather | solution.py:49
  1763.7 24.8 %multiply_convert_fusion = bf16[16384,768]{1,0:T(8,128)(2,1)} fusion(bf16[16384,768]{1,0:T(8,128)(2,1)} %gather_fusion.1, f32[16384]{0:T(1024)S(1)} %bitcast.53, pred[16384]{0:T(1024)(128)(4,1)S(1)} %copy-done.4), kind=kLoop, calls=%fused_computation.12 | loop fusion | flops 50331648 | bytes 50413568 | tf_op jit(solution)/shard_map/convert_element_type | solution.py:51
  (15 shorter events, 0.1 us)
Async XLA Ops:
  6.5 485.2 %copy-start = (bf16[2,768,768]{2,1,0:T(8,128)(2,1)S(1)}, bf16[2,768,768]{2,1,0:T(8,128)(2,1)}, u32[]{:S(2)}) copy-start(bf16[2,768,768]{2,1,0:T(8,128)(2,1)} %param.9) | copy-start | bytes 7077892
  6.6 485.2 %all-gather.3.cloned.1.call-start = ((), (), s32[]{:S(2)}) async-start(), calls=%async_computation.3 | async-start | bytes 39321600 | tf_op jit(solution)/shard_map/all_gather | solution.py:41
  216.2 856.7 %reduce-scatter.2.cloned.1.call-start = ((), (), s32[]{:S(2)}) async-start(), calls=%async_computation.4 | async-start | bytes 78643200 | tf_op jit(solution)/shard_map/reduce_scatter | solution.py:45
  555.1 901.1 %all-gather.5.cloned.1.call-start = ((), (), s32[]{:S(2)}) async-start(), calls=%async_computation.5 | async-start | bytes 39321600 | tf_op jit(solution)/shard_map/all_gather | solution.py:47
  1082.6 101.4 %copy-start.2 = (s32[16384,1]{0,1:T(1,128)S(1)}, s32[16384,1]{0,1:T(1,128)}, u32[]{:S(2)}) copy-start(s32[16384,1]{0,1:T(1,128)} %get-tuple-element.6) | copy-start | bytes 196612
  1477.8 285.9 %copy-start.3 = (f32[16384,1]{0,1:T(1,128)S(1)}, f32[16384,1]{0,1:T(1,128)}, u32[]{:S(2)}) copy-start(f32[16384,1]{0,1:T(1,128)} %param.7) | copy-start | bytes 196612
  1477.8 285.9 %copy-start.4 = (pred[16384]{0:T(1024)(128)(4,1)S(1)}, pred[16384]{0:T(1024)(128)(4,1)}, u32[]{:S(2)}) copy-start(pred[16384]{0:T(1024)(128)(4,1)} %get-tuple-element.5) | copy-start | bytes 49156
  1763.7 24.8 %copy-start.1 = (bf16[2,768,768]{2,1,0:T(8,128)(2,1)S(1)}, bf16[2,768,768]{2,1,0:T(8,128)(2,1)}, u32[]{:S(2)}) copy-start(bf16[2,768,768]{2,1,0:T(8,128)(2,1)} %param.9) | copy-start | bytes 7077892
Sparse Core Ops, SparseCore 0:
  216.4 275.2 all-gather.2
  555.2 517.6 reduce-scatter.1
  1184.1 272.0 all-gather.4
where the time goes:
time: 1800 us
  waiting for transfers between devices  1070 us (59%)
  local copies, waits for them, and re-layouts  420 us (23%)
  blocking collectives  188 us (10%)
  matrix products  63.4 us (4%)
  other arithmetic  45 us (2%)
    reduce_scatter x1, waiting for transfers between devices, local_moe(): lax.psum_scatter(part_out, 'tp', scatter_dimension=2, tiled=True)  518 us
    gather x1, local copies, waits for them, and re-layouts, local_moe(): picked = jnp.take(own_out, out_pos, axis=0, mode='fill', fill_value=0)  286 us
    all_gather x1, waiting for transfers between devices, local_moe(): expert_in = lax.all_gather(arrived, 'tp', axis=2, tiled=True)  275 us
    all_gather x1, waiting for transfers between devices, local_moe(): lax.all_gather(returned, 'tp', axis=2, tiled=True)  272 us
    all_to_all x1, blocking collectives, local_moe(): returned = lax.all_to_all(expert_out, 'ep', 1, 1, tiled=True)  94.3 us
    all_to_all x1, blocking collectives, local_moe(): arrived = lax.all_to_all(outgoing, 'ep', 1, 1, tiled=True)  93.8 us
    dot_general x1, matrix products, local_moe(): jnp.einsum('escf,efd->escd', hidden_act, w_out, preferred_element_type=jn...  63.4 us
    scatter x1, local copies, waits for them, and re-layouts, local_moe(): jnp.full((n_send + 1,), tokens, jnp.int32).at[send_pos].set(tok_ids)  60.4 us
  transfers between devices with their start and end apart: 3, of which 3 were waited for; matrix products, arithmetic and copies ran while one was open for 0% of the time, Pallas kernels for 0%

commit v1 on v0

v1 whole, which is shorter than its diff:
```python
import functools

import jax
import jax.numpy as jnp
from jax import lax
from jax.experimental import pallas as pl
from jax.experimental.pallas import tpu as pltpu
from jax.sharding import PartitionSpec as P

LANES = 128
WIN = 16
BLOCK = 256
ROW_TILE = 256
COL_SPAN = 1024
SHARES = (2, 5, 8, 5)


def capacity_of(top_k, tokens, experts, tp_size):
    divisor = 32 * experts * tp_size
    return 8 * tp_size * ((5 * top_k * tokens + divisor - 1) // divisor)


def tri(n, inclusive):
    rows = lax.broadcasted_iota(jnp.int32, (n, n), 0)
    cols = lax.broadcasted_iota(jnp.int32, (n, n), 1)
    return (rows <= cols if inclusive else rows < cols).astype(jnp.bfloat16)


def int_dot(spec, a, b):
    return jnp.einsum(spec, a.astype(jnp.bfloat16), b.astype(jnp.bfloat16), preferred_element_type=jnp.float32)


def ffn_kernel(x_ref, *refs):
    w_refs, out_ref = refs[:8], refs[-1]
    x = x_ref[...]
    total = None
    for shard in range(4):
        pre = jnp.dot(x, w_refs[shard][...], preferred_element_type=jnp.float32)
        act = jax.nn.gelu(pre, approximate=True).astype(jnp.bfloat16)
        part = jnp.dot(act, w_refs[4 + shard][...], preferred_element_type=jnp.float32)
        total = part if total is None else total + part
    out_ref[...] = total.astype(out_ref.dtype)


def ffn(x, w_ins, w_outs, after):
    rows, hidden = x.shape
    width = w_ins[0].shape[1]
    fixed = lambda i: (0, 0)
    specs = [pl.BlockSpec((ROW_TILE, hidden), lambda i: (i, 0))]
    specs += [pl.BlockSpec((hidden, width), fixed)] * 4 + [pl.BlockSpec((width, hidden), fixed)] * 4
    specs += [pl.BlockSpec(memory_space=pl.ANY)] * len(after)
    return pl.pallas_call(
        ffn_kernel,
        grid=(rows // ROW_TILE,),
        in_specs=specs,
        out_specs=pl.BlockSpec((ROW_TILE, hidden), lambda i: (i, 0)),
        out_shape=jax.ShapeDtypeStruct((rows, hidden), jnp.bfloat16),
        compiler_params=pltpu.CompilerParams(dimension_semantics=("arbitrary",), vmem_limit_bytes=60 * 2**20),
        cost_estimate=pl.CostEstimate(flops=16 * rows * hidden * width, bytes_accessed=4 * rows * hidden + 16 * hidden * width, transcendentals=4 * rows * width),
        name="ffn",
    )(x, *w_ins, *w_outs, *after)


def combine_kernel(chunk, active_ref, count_ref, src_ref, table, col_ref, gate_ref, *refs):
    first = chunk == 0
    old_hbm, refs = (None, refs) if first else (refs[0], refs[1:])
    out_hbm, held, old_buf, out_buf, acc, win_sem, old_sem, out_sem = refs
    steps = count_ref.shape[0]
    n_active = active_ref[steps]

    def rows_of(block):
        return pl.ds(pl.multiple_of(block * BLOCK, BLOCK), BLOCK)

    def window(block, slot, w):
        row = pl.multiple_of(src_ref[block, w] * WIN, WIN)
        return pltpu.make_async_copy(table.at[pl.ds(row, WIN), :], held.at[slot, pl.ds(pl.multiple_of(w * WIN, WIN), WIN), :], win_sem.at[slot, w])

    def earlier(block, slot):
        return pltpu.make_async_copy(old_hbm.at[rows_of(block), :], old_buf.at[slot], old_sem.at[slot])

    def output(block, slot):
        return pltpu.make_async_copy(out_buf.at[slot], out_hbm.at[rows_of(block), :], out_sem.at[slot])

    def fetch(i, slot):
        block = active_ref[i]
        if not first:
            earlier(block, slot).start()

        def issue(w, _):
            window(block, slot, w).start()
            return 0

        lax.fori_loop(0, count_ref[block], issue, 0)

    held[...] = jnp.zeros_like(held)

    @pl.when(n_active > 0)
    def _():
        fetch(0, 0)

    def body(i, _):
        slot = i % 2
        block = active_ref[i]

        @pl.when(i + 1 < n_active)
        def _():
            fetch(i + 1, 1 - slot)

        if not first:
            earlier(block, slot).wait()
        n = count_ref[block]

        def land(w, _):
            window(block, slot, w).wait()
            return 0

        lax.fori_loop(0, n, land, 0)

        @pl.when(i >= 2)
        def _():
            output(active_ref[i - 2], slot).wait()

        def down(ref):
            return jnp.broadcast_to(ref[pl.ds(block, 1), :], (LANES, BLOCK)).T

        depth = 2 * LANES
        lane = lax.broadcasted_iota(jnp.int32, (BLOCK, LANES), 1).astype(jnp.float32)
        col = down(col_ref) - chunk * COL_SPAN - lane

        def part(k):
            at = lax.convert_element_type(k * depth, jnp.float32)
            pick = jnp.concatenate([(col == at + LANES * j).astype(jnp.float32).astype(jnp.bfloat16) for j in range(2)], axis=1)
            return jnp.dot(pick, held[slot, pl.ds(pl.multiple_of(k * depth, depth), depth), :], preferred_element_type=jnp.float32)

        acc[...] = part(0)

        def more(k, _):
            acc[...] += part(k)
            return 0

        lax.fori_loop(1, (n * WIN + depth - 1) // depth, more, 0)
        gate = down(gate_ref)
        for k in range(acc.shape[1] // LANES):
            cut = slice(k * LANES, (k + 1) * LANES)
            new = acc[:, cut] * gate
            if not first:
                new = new + old_buf[slot, :, cut].astype(jnp.float32)
            out_buf[slot, :, cut] = new.astype(out_buf.dtype)
        output(block, slot).start()
        return 0

    lax.fori_loop(0, n_active, body, 0)

    @pl.when(n_active > 1)
    def _():
        output(active_ref[n_active - 2], n_active % 2).wait()

    @pl.when(n_active > 0)
    def _():
        output(active_ref[n_active - 1], (n_active - 1) % 2).wait()


def combine(chunk, n_win, active, count, src, table, col, gate, old):
    tokens, hidden = col.size, table.shape[1]
    smem, any_ = pl.BlockSpec(memory_space=pltpu.SMEM), pl.BlockSpec(memory_space=pl.ANY)
    olds = [] if old is None else [old]
    block = lambda width, dtype: pltpu.VMEM((2, BLOCK, width), dtype)
    return pl.pallas_call(
        functools.partial(combine_kernel, chunk),
        in_specs=[smem] * 3 + [any_] + [pl.BlockSpec(memory_space=pltpu.VMEM)] * 2 + [any_] * len(olds),
        out_specs=any_,
        out_shape=jax.ShapeDtypeStruct((tokens, hidden), jnp.bfloat16),
        input_output_aliases={6: 0} if olds else {},
        scratch_shapes=[
            pltpu.VMEM((2, n_win * WIN, hidden), jnp.bfloat16),
            block(hidden, jnp.bfloat16),
            block(hidden, jnp.bfloat16),
            pltpu.VMEM((BLOCK, hidden), jnp.float32),
            pltpu.SemaphoreType.DMA((2, n_win)),
            pltpu.SemaphoreType.DMA((2,)),
            pltpu.SemaphoreType.DMA((2,)),
        ],
        compiler_params=pltpu.CompilerParams(vmem_limit_bytes=60 * 2**20),
        cost_estimate=pl.CostEstimate(flops=tokens * n_win * WIN * hidden, bytes_accessed=2 * tokens * hidden, transcendentals=0),
        name="combine",
    )(active, count, src, table, col, gate, *olds)


def solution(mesh):
    tp_size = mesh.shape["tp"]
    ep_size = mesh.shape["ep"]
    assert tp_size == 4

    def whole_moe(act_loc, idx_loc, gate_loc, w_in, w_out):
        tokens, hidden = act_loc.shape
        local_experts = w_in.shape[0]
        assert idx_loc.shape[1] == 1 and local_experts == 2
        experts = local_experts * ep_size
        capacity = capacity_of(1, tokens, experts, tp_size)
        shares = tp_size // local_experts
        chunks = len(SHARES)
        pieces = [capacity // shares * n // sum(SHARES) for n in SHARES]
        heads = [shares * sum(pieces[:q]) for q in range(chunks)]
        assert shares * sum(pieces) == capacity and all(ep_size * p % ROW_TILE == 0 and p % WIN == 0 for p in pieces)
        assert tokens % BLOCK == 0 and BLOCK % LANES == 0
        rank = lax.axis_index("tp")
        which = rank // shares

        twin = [(i, i ^ 1) for i in range(tp_size)]
        mirror = [(i, tp_size - 1 - i) for i in range(tp_size)]
        w_ins, w_outs = [], []
        for whole, kept in ((w_in, w_ins), (w_out, w_outs)):
            mine = lax.dynamic_index_in_dim(whole, which, 0, keepdims=False)
            other = lax.dynamic_index_in_dim(whole, 1 - which, 0, keepdims=False)
            across = lax.ppermute(other, "tp", mirror)
            near = lax.ppermute(mine, "tp", twin)
            far = lax.ppermute(across, "tp", twin)
            kept += [mine, near, across, far]

        blocks = tokens // LANES
        chosen = idx_loc.reshape(blocks, LANES)
        hits = chosen[None] == jnp.arange(experts, dtype=jnp.int32)[:, None, None]
        within = int_dot("ebi,ij->ebj", hits, tri(LANES, True))
        totals = within[:, :, LANES - 1]
        base = int_dot("eb,bc->ec", totals, tri(blocks, False))
        upto = base + totals
        slot = jnp.sum(jnp.where(hits, base[:, :, None] + within - 1, 0.0), axis=0).astype(jnp.int32)

        mine_of = lambda a: lax.dynamic_index_in_dim(a.reshape((ep_size, local_experts) + a.shape[1:]), which, 1, keepdims=False)
        my_within, my_base, my_upto = mine_of(within), mine_of(base), mine_of(upto)
        my_slot = jnp.concatenate([heads[q] + (rank % shares) * pieces[q] + jnp.arange(pieces[q], dtype=jnp.int32) for q in range(chunks)])
        my_slot = my_slot.astype(jnp.float32)
        in_block = jnp.sum((my_upto[:, None, :] <= my_slot[None, :, None]).astype(jnp.int32), axis=2)
        is_block = in_block[:, :, None] == jnp.arange(blocks, dtype=jnp.int32)
        row_within = int_dot("dsb,dbi->dsi", is_block, my_within)
        row_base = jnp.sum(jnp.where(is_block, my_base[:, None, :], 0.0), axis=2)
        in_row = jnp.sum((row_within <= (my_slot[None, :] - row_base)[:, :, None]).astype(jnp.int32), axis=2)
        tok = jnp.where(in_block < blocks, in_block * LANES + in_row, tokens)

        n_win = -(-(BLOCK + experts * 2 * (WIN - 1)) // WIN)
        n_win = -(-n_win * WIN // LANES) * LANES // WIN
        steps = tokens // BLOCK
        first = jnp.minimum(base[:, :: BLOCK // LANES], capacity).astype(jnp.int32).T
        last = jnp.minimum(upto[:, BLOCK // LANES - 1 :: BLOCK // LANES], capacity).astype(jnp.int32).T
        win_lo = first // WIN
        win_hi = jnp.where(last > first, (last - 1) // WIN + 1, win_lo)
        of_slot = lambda per_chunk, at: sum((per_chunk[q] - per_chunk[q - 1]) * (at >= heads[q]).astype(jnp.int32) if q else per_chunk[0] for q in range(chunks))
        edge = jnp.asarray([h // WIN for h in heads] + [capacity // WIN], jnp.int32)
        lo = jnp.maximum(win_lo[:, None, :], edge[None, :-1, None])
        count = jnp.maximum(jnp.minimum(win_hi[:, None, :], edge[None, 1:, None]) - lo, 0)
        ends = int_dot("sqe,ef->sqf", count, tri(experts, True)).astype(jnp.int32)
        starts = ends - count
        n_fetch = ends[:, :, experts - 1].T
        w_id = jnp.arange(n_win, dtype=jnp.int32)
        of_expert = jnp.sum((ends[:, :, None, :] <= w_id[None, None, :, None]).astype(jnp.int32), axis=3)
        is_expert = of_expert[:, :, :, None] == jnp.arange(experts, dtype=jnp.int32)
        win = jnp.sum(jnp.where(is_expert, (lo - starts)[:, :, None, :], 0), axis=3) + w_id - edge[None, :-1, None]
        per_piece = jnp.asarray([p // WIN for p in pieces], jnp.int32)[None, :, None]
        share_of = (win >= per_piece).astype(jnp.int32) if shares == 2 else win // per_piece
        of_rank = (of_expert % local_experts) * shares + share_of
        src = (of_rank * ep_size + of_expert // local_experts) * per_piece + win - share_of * per_piece
        src = jnp.where(of_expert < experts, src, 0)
        busy = (n_fetch > 0) | (jnp.arange(chunks)[:, None] == 0)
        before = int_dot("qs,st->qt", busy, tri(steps, True)).astype(jnp.int32)
        nth = jnp.arange(steps + 1, dtype=jnp.int32)
        active = jnp.sum((before[:, None, :] <= nth[None, :, None]).astype(jnp.int32), axis=2)
        active = jnp.where(nth[None] == steps, before[:, -1:], active)
        slot_rows = slot.reshape(steps, BLOCK)
        pair_of = of_slot([q * experts for q in range(chunks)], slot_rows) + idx_loc.reshape(steps, BLOCK)
        pairs = chunks * experts
        move = ((starts - lo) * WIN + jnp.arange(chunks, dtype=jnp.int32)[None, :, None] * COL_SPAN).reshape(steps, 1, pairs)
        shift = jnp.sum(jnp.where(pair_of[:, :, None] == jnp.arange(pairs, dtype=jnp.int32), move, 0), axis=2)
        col = jnp.where(slot_rows < capacity, slot_rows + shift, -1).astype(jnp.float32)
        gate = gate_loc.reshape(steps, BLOCK)

        def exchange(rows):
            return lax.all_to_all(rows.reshape(ep_size, -1, hidden), "ep", 0, 0, tiled=True)

        outgoing = []
        for q in range(chunks):
            at = sum(pieces[:q])
            rows = tok[:, at : at + pieces[q]].reshape(-1)
            outgoing.append(jnp.take(act_loc, rows, axis=0, mode="fill", fill_value=0))
        arrived = [exchange(outgoing[q]) for q in range(chunks - 1)]
        made, returned = [], []
        for q in range(chunks):
            if q == chunks - 1:
                outgoing[q], returned[q - 1] = lax.optimization_barrier((outgoing[q], returned[q - 1]))
                arrived.append(exchange(outgoing[q]))
            made.append(ffn(arrived[q].reshape(-1, hidden), w_ins, w_outs, made[q - 1 : q] if q else [outgoing[chunks - 1], arrived[1]]))
            if q == chunks - 1:
                made[q], col, gate, src, n_fetch, active = lax.optimization_barrier((made[q], col, gate, src, n_fetch, active))
            returned.append(exchange(made[q]))
        tables = [lax.all_gather(r, "tp", axis=0).reshape(-1, hidden) for r in returned]
        out = None
        for q in range(chunks):
            out = combine(q, n_win, active[q], n_fetch[q], src[:, q, :], tables[q], col, gate, out)
        return out

    tok_spec = P(("dp", "ep"), None)
    return jax.shard_map(whole_moe, mesh=mesh, in_specs=(tok_spec, tok_spec, tok_spec, P("ep", None, "tp"), P("ep", "tp", None)), out_specs=tok_spec, check_vma=False)
```

time: 1800 us -> 616 us (0.34)
  waiting for transfers between devices: 1070 us -> 101 us
  local copies, waits for them, and re-layouts: 420 us -> 79.9 us
  Pallas kernels: 0 us -> 211 us
  matrix products: 63.4 us -> 2.55 us
  other arithmetic: 45 us -> 12.6 us
  blocking collectives: 188 us -> 163 us
  starting transfers between devices: 0.53 us -> 24.4 us
    all_gather x2 -> x4, waiting for transfers between devices: 547 us -> 0.06 us  [whole_moe(): lax.all_gather(r, 'tp', axis=0).reshape(-1, hidden)]
    reduce_scatter x1 -> x0, waiting for transfers between devices: 518 us -> none  [local_moe(): lax.psum_scatter(part_out, 'tp', scatter_dimension=2, tiled=True)]
    gather x2 -> x4, local copies, waits for them, and re-layouts: 321 us -> 67.9 us  [whole_moe(): outgoing.append(jnp.take(act_loc, rows, axis=0, mode='fill', fill_value=0))]
    pallas_call x0 -> x8, Pallas kernels: none -> 211 us  [the longest x4 133 us: combine(): pl.pallas_call(functools.partial(combine_kernel, chunk), in_specs=[smem]...]
    ppermute x0 -> x6, waiting for transfers between devices: none -> 82.2 us  [the longest x2 50.6 us: whole_moe(): far = lax.ppermute(across, 'tp', twin)]
    dot_general x1 -> x5, matrix products: 63.4 us -> 2.55 us  [int_dot(): jnp.einsum(spec, a.astype(jnp.bfloat16), b.astype(jnp.bfloat16), preferre...]
    scatter x1 -> x0, local copies, waits for them, and re-layouts: 60.4 us -> none  [local_moe(): jnp.full((n_send + 1,), tokens, jnp.int32).at[send_pos].set(tok_ids)]
    convert_element_type x2 -> x3, other arithmetic: 34.5 us -> 0.75 us  [the longest x1 0.65 us: whole_moe(): jnp.where(slot_rows < capacity, slot_rows + shift, -1).astype(jnp.float32)]
  transfers between devices with their start and end apart: 3 -> 13, of which waited for: 3 -> 5; matrix products, arithmetic and copies ran while one was open for 0% -> 15% of each run, Pallas kernels for 0% -> 32%
where the time goes in v1:
time: 616 us; the launch traced here: 608 us
  Pallas kernels  211 us (34%)
  blocking collectives  163 us (26%)
  waiting for transfers between devices  101 us (16%)
  local copies, waits for them, and re-layouts  79.9 us (13%)
  starting transfers between devices  24.4 us (4%)
  between operations  13.9 us (2%)
  other arithmetic  12.6 us (2%)
    all_to_all x5, blocking collectives, exchange(): lax.all_to_all(rows.reshape(ep_size, -1, hidden), 'ep', 0, 0, tiled=True)  163 us
    pallas_call x4, Pallas kernels, combine(): pl.pallas_call(functools.partial(combine_kernel, chunk), in_specs=[smem]...  133 us
    pallas_call x4, Pallas kernels, ffn(): pl.pallas_call(ffn_kernel, grid=(rows // ROW_TILE,), in_specs=specs, out_...  78.3 us
    gather x4, local copies, waits for them, and re-layouts, whole_moe(): outgoing.append(jnp.take(act_loc, rows, axis=0, mode='fill', fill_value=0))  67.9 us
    ppermute x2, waiting for transfers between devices, whole_moe(): far = lax.ppermute(across, 'tp', twin)  50.6 us
    ppermute x2, waiting for transfers between devices, whole_moe(): near = lax.ppermute(mine, 'tp', twin)  31.7 us
    all_to_all x3, waiting for transfers between devices, exchange(): lax.all_to_all(rows.reshape(ep_size, -1, hidden), 'ep', 0, 0, tiled=True)  18.4 us
    all_to_all x3, starting transfers between devices, exchange(): lax.all_to_all(rows.reshape(ep_size, -1, hidden), 'ep', 0, 0, tiled=True)  15.6 us
  transfers between devices with their start and end apart: 13, of which 5 were waited for; matrix products, arithmetic and copies ran while one was open for 15% of the time, Pallas kernels for 32%

profile of v1, /device:TPU:97, one launch (start us, length us, event | category | flops | bytes accessed | tf_op | source)
XLA Modules:
  0.0 608.3 jit_solution(5904136363005107643)
XLA Ops:
  6.5 3.0 dynamic-slice_bitcast_fusion.2
  9.6 5.2 collective-permute-start.1
  14.7 1.5 dynamic-slice_bitcast_fusion
  18.8 1.8 select_reduce_fusion.1
  20.6 1.7 fusion.2
  22.8 13.8 %gather_fusion.1 = bf16[512,768]{1,0:T(8,128)(2,1)S(1)} fusion(bf16[16384,768]{1,0:T(8,128)(2,1)} %param.9, s32[1024]{0:T(1024)S(1)} %pad_clamp_fusion.2), kind=kCustom, calls=%fused_computation.3 | custom fusion | bytes 1574912 | tf_op jit(solution)/shard_map/jit(_take)/gather | solution.py:283
  37.7 6.1 all-to-all-start.2
  43.9 16.6 %gather_fusion.3 = bf16[1280,768]{1,0:T(8,128)(2,1)S(1)} fusion(bf16[16384,768]{1,0:T(8,128)(2,1)} %param.9, s32[2048]{0:T(1024)S(1)} %pad_clamp_fusion), kind=kCustom, calls=%fused_computation.1.clone | custom fusion | bytes 3937280 | tf_op jit(solution)/shard_map/jit(_take)/gather | solution.py:283
  60.5 1.5 broadcast_select_fusion.1
  62.0 4.8 all-to-all-start.1
  70.0 16.6 %gather_fusion.2 = bf16[1280,768]{1,0:T(8,128)(2,1)S(1)} fusion(bf16[16384,768]{1,0:T(8,128)(2,1)} %param.9, s32[2048]{0:T(1024)S(1)} %pad_clamp_fusion.1), kind=kCustom, calls=%fused_computation.clone | custom fusion | bytes 3937280 | tf_op jit(solution)/shard_map/jit(_take)/gather | solution.py:283
  86.6 1.6 broadcast_select_fusion.2.refs_8_
  88.1 6.4 %collective-permute-done.refs_1_ = bf16[768,768]{1,0:T(8,128)(2,1)} collective-permute-done((bf16[768,768]{1,0:T(8,128)(2,1)S(1)}, bf16[768,768]{1,0:T(8,128)(2,1)}, u32[]{:S(2)}, u32[]{:S(2)}) %collective-permute-start) | collective-permute-done | bytes 1179680 | tf_op jit(solution)/shard_map/ppermute | solution.py:216
  94.5 25.3 %collective-permute-done.3.refs_5_ = bf16[768,768]{1,0:T(8,128)(2,1)} collective-permute-done((bf16[768,768]{1,0:T(8,128)(2,1)}, bf16[768,768]{1,0:T(8,128)(2,1)}, u32[]{:S(2)}, u32[]{:S(2)}) %collective-permute-start.3) | collective-permute-done | bytes 1179680 | tf_op jit(solution)/shard_map/ppermute | solution.py:216
  119.8 25.3 %collective-permute-done.2.refs_3_ = bf16[768,768]{1,0:T(8,128)(2,1)} collective-permute-done((bf16[768,768]{1,0:T(8,128)(2,1)}, bf16[768,768]{1,0:T(8,128)(2,1)}, u32[]{:S(2)}, u32[]{:S(2)}) %collective-permute-start.2) | collective-permute-done | bytes 1179680 | tf_op jit(solution)/shard_map/ppermute | solution.py:217
  145.1 25.3 %collective-permute-done.5.refs_7_ = bf16[768,768]{1,0:T(8,128)(2,1)} collective-permute-done((bf16[768,768]{1,0:T(8,128)(2,1)}, bf16[768,768]{1,0:T(8,128)(2,1)}, u32[]{:S(2)}, u32[]{:S(2)}) %collective-permute-start.5) | collective-permute-done | bytes 1179680 | tf_op jit(solution)/shard_map/ppermute | solution.py:217
  170.3 10.5 %ffn.4.refs_8_ = bf16[512,768]{1,0:T(8,128)(2,1)} custom-call(bf16[512,768]{1,0:T(8,128)(2,1)} %bitcast.20.x_ref, bf16[768,768]{1,0:T(8,128)(2,1)} %copy-done.4, bf16[768,768]{1,0:T(8,128)(2,1)} %collective-permute-done.refs_1_, bf16[768,768]{1,0:T(8,128)(2,1)} %collective-permute-done.1.refs_2_, bf16[768,768]{1,0:T(8,128)(2,1)} %collective-permute-done.2.refs_3_, ...), custom_call_target="tpu_custom_call" | custom-call | flops 4831838208 | bytes 11010048 | tf_op jit(solution)/shard_map/ffn/pallas_call | solution.py:52
  180.9 17.6 %all_to_all.40 = bf16[8,64,768]{2,1,0:T(8,128)(2,1)} all-to-all(bf16[8,64,768]{2,1,0:T(8,128)(2,1)} %bitcast.127), channel_id=1, replica_groups=mesh['dp'=1,'tp'=4,'ep'=8] {'ep'}, dimensions={0} | all-to-all | bytes 1572864 | tf_op jit(solution)/shard_map/all_to_all | solution.py:277
  198.6 19.6 %ffn.5.refs_8_ = bf16[1280,768]{1,0:T(8,128)(2,1)} custom-call(bf16[1280,768]{1,0:T(8,128)(2,1)} %bitcast.17.x_ref, bf16[768,768]{1,0:T(8,128)(2,1)} %copy-done.4, bf16[768,768]{1,0:T(8,128)(2,1)} %collective-permute-done.refs_1_, bf16[768,768]{1,0:T(8,128)(2,1)} %collective-permute-done.1.refs_2_, bf16[768,768]{1,0:T(8,128)(2,1)} %collective-permute-done.2.refs_3_, ...), custom_call_target="tpu_custom_call" | custom-call | flops 12079595520 | bytes 13369344 | tf_op jit(solution)/shard_map/ffn/pallas_call | solution.py:52
  218.2 30.4 %all_to_all.41 = bf16[8,160,768]{2,1,0:T(8,128)(2,1)} all-to-all(bf16[8,160,768]{2,1,0:T(8,128)(2,1)} %bitcast.125), channel_id=1, replica_groups=mesh['dp'=1,'tp'=4,'ep'=8] {'ep'}, dimensions={0} | all-to-all | bytes 3932160 | tf_op jit(solution)/shard_map/all_to_all | solution.py:277
  249.0 21.0 %gather_fusion = bf16[2048,768]{1,0:T(8,128)(2,1)S(1)} fusion(bf16[16384,768]{1,0:T(8,128)(2,1)} %param.9, s32[2048]{0:T(1024)S(1)} %broadcast_clamp_fusion), kind=kCustom, calls=%fused_computation.2 | custom fusion | bytes 6299648 | tf_op jit(solution)/shard_map/jit(_take)/gather | solution.py:283
  270.5 41.7 %all_to_all.42 = bf16[8,256,768]{2,1,0:T(8,128)(2,1)} all-to-all(bf16[8,256,768]{2,1,0:T(8,128)(2,1)S(1)} %broadcast_select_fusion), channel_id=1, replica_groups=mesh['dp'=1,'tp'=4,'ep'=8] {'ep'}, dimensions={0} | all-to-all | bytes 6291456 | tf_op jit(solution)/shard_map/all_to_all | solution.py:277
  312.2 28.5 %ffn.6.refs_8_ = bf16[2048,768]{1,0:T(8,128)(2,1)} custom-call(bf16[2048,768]{1,0:T(8,128)(2,1)} %bitcast.122, bf16[768,768]{1,0:T(8,128)(2,1)} %copy-done.4, bf16[768,768]{1,0:T(8,128)(2,1)} %collective-permute-done.refs_1_, bf16[768,768]{1,0:T(8,128)(2,1)} %collective-permute-done.1.refs_2_, bf16[768,768]{1,0:T(8,128)(2,1)} %collective-permute-done.2.refs_3_, ...), custom_call_target="tpu_custom_call" | custom-call | flops 19327352832 | bytes 15728640 | tf_op jit(solution)/shard_map/ffn/pallas_call | solution.py:52
  340.7 43.0 %all_to_all.43 = bf16[8,256,768]{2,1,0:T(8,128)(2,1)} all-to-all(bf16[8,256,768]{2,1,0:T(8,128)(2,1)} %bitcast.121), channel_id=1, replica_groups=mesh['dp'=1,'tp'=4,'ep'=8] {'ep'}, dimensions={0} | all-to-all | bytes 6291456 | tf_op jit(solution)/shard_map/all_to_all | solution.py:277
  385.8 4.7 all-to-all-start.4
  397.0 18.4 %all-to-all-done.4 = bf16[8,160,768]{2,1,0:T(8,128)(2,1)S(1)} async-done(((bf16[8,160,768]{2,1,0:T(8,128)(2,1)}), bf16[8,160,768]{2,1,0:T(8,128)(2,1)S(1)}, u32[]{:S(2)}, u32[]{:S(2)}) %all-to-all-start.4) | async-done | bytes 1966112 | tf_op jit(solution)/shard_map/all_to_all | solution.py:277
  416.6 19.7 %ffn.7 = bf16[1280,768]{1,0:T(8,128)(2,1)} custom-call(bf16[1280,768]{1,0:T(8,128)(2,1)} %bitcast.124, bf16[768,768]{1,0:T(8,128)(2,1)} %copy-done.4, bf16[768,768]{1,0:T(8,128)(2,1)} %collective-permute-done.refs_1_, bf16[768,768]{1,0:T(8,128)(2,1)} %collective-permute-done.1.refs_2_, bf16[768,768]{1,0:T(8,128)(2,1)} %collective-permute-done.2.refs_3_, ...), custom_call_target="tpu_custom_call" | custom-call | flops 12079595520 | bytes 13369344 | tf_op jit(solution)/shard_map/ffn/pallas_call | solution.py:52
  436.3 30.3 %all_to_all.44 = bf16[8,160,768]{2,1,0:T(8,128)(2,1)} all-to-all(bf16[8,160,768]{2,1,0:T(8,128)(2,1)} %bitcast.126), channel_id=1, replica_groups=mesh['dp'=1,'tp'=4,'ep'=8] {'ep'}, dimensions={0} | all-to-all | bytes 3932160 | tf_op jit(solution)/shard_map/all_to_all | solution.py:277
  468.5 46.6 %combine.4.refs_0_ = bf16[16384,768]{1,0:T(8,128)(2,1)} custom-call(s32[65]{0:T(128)} %get-tuple-element.40.active_ref, s32[64]{0:T(128)} %get-tuple-element.36.count_ref, s32[64,48]{1,0:T(8,128)} %get-tuple-element.26.src_ref, bf16[2048,768]{1,0:T(8,128)(2,1)} %bitcast.140, f32[64,256]{1,0:T(8,128)} %select_convert_fusion.col_ref, f32[64,256]{1,0:T(8,128)} %reshape.285.gate_ref), custom_call_target="tpu_custom_call" | custom-call | flops 9663676416 | bytes 25165824 | tf_op jit(solution)/shard_map/combine/pallas_call | solution.py:168
  515.2 32.5 %combine.5.refs_0_ = bf16[16384,768]{1,0:T(8,128)(2,1)} custom-call(s32[65]{0:T(128)} %get-tuple-element.41.active_ref, s32[64]{0:T(128)} %get-tuple-element.37.count_ref, s32[64,48]{1,0:T(8,128)} %get-tuple-element.27.src_ref, bf16[5120,768]{1,0:T(8,128)(2,1)} %bitcast.118, f32[64,256]{1,0:T(8,128)} %select_convert_fusion.col_ref, ...), custom_call_target="tpu_custom_call", output_to_operand_aliasing={{}: (6, {})} | custom-call | flops 9663676416 | bytes 25165824 | tf_op jit(solution)/shard_map/combine/pallas_call | solution.py:168
  547.7 46.1 %combine.6.refs_0_ = bf16[16384,768]{1,0:T(8,128)(2,1)} custom-call(s32[65]{0:T(128)} %get-tuple-element.42.active_ref, s32[64]{0:T(128)} %get-tuple-element.38.count_ref, s32[64,48]{1,0:T(8,128)} %get-tuple-element.28.src_ref, bf16[8192,768]{1,0:T(8,128)(2,1)} %bitcast.117, f32[64,256]{1,0:T(8,128)} %select_convert_fusion.col_ref, ...), custom_call_target="tpu_custom_call", output_to_operand_aliasing={{}: (6, {})} | custom-call | flops 9663676416 | bytes 25165824 | tf_op jit(solution)/shard_map/combine/pallas_call | solution.py:168
  593.9 7.6 %combine.7 = bf16[16384,768]{1,0:T(8,128)(2,1)} custom-call(s32[65]{0:T(128)} %get-tuple-element.43.active_ref, s32[64]{0:T(128)} %get-tuple-element.39.count_ref, s32[64,48]{1,0:T(8,128)} %get-tuple-element.29.src_ref, bf16[5120,768]{1,0:T(8,128)(2,1)} %bitcast.119, f32[64,256]{1,0:T(8,128)} %select_convert_fusion.col_ref, ...), custom_call_target="tpu_custom_call", output_to_operand_aliasing={{}: (6, {})} | custom-call | flops 9663676416 | bytes 25165824 | tf_op jit(solution)/shard_map/combine/pallas_call | solution.py:168
  (115 shorter events, 20.0 us)
Async XLA Ops:
  6.5 8.2 %copy-start.2 = (bf16[2,768,768]{2,1,0:T(8,128)(2,1)S(1)}, bf16[2,768,768]{2,1,0:T(8,128)(2,1)}, u32[]{:S(2)}) copy-start(bf16[2,768,768]{2,1,0:T(8,128)(2,1)} %param.13) | copy-start | bytes 7077892
  9.6 57.3 %copy-start.4 = (bf16[768,768]{1,0:T(8,128)(2,1)}, bf16[768,768]{1,0:T(8,128)(2,1)S(1)}, u32[]{:S(2)}) copy-start(bf16[768,768]{1,0:T(8,128)(2,1)S(1)} %get-tuple-element.25.refs_0_) | copy-start | bytes 3538948
  9.6 58.9 %collective-permute-start.1 = (bf16[768,768]{1,0:T(8,128)(2,1)}, bf16[768,768]{1,0:T(8,128)(2,1)}, u32[]{:S(2)}, u32[]{:S(2)}) collective-permute-start(bf16[768,768]{1,0:T(8,128)(2,1)} %get-tuple-element.24), channel_id=1, source_target_pairs={{0,24},{8,16},{16,8},{24,0},{1,25},{9,17},{17,9},{25,1},{2,26},{10... | collective-permute-start | bytes 3538952 | tf_op jit(solution)/shard_map/ppermute | solution.py:215
  16.3 52.3 %collective-permute-start.4 = (bf16[768,768]{1,0:T(8,128)(2,1)}, bf16[768,768]{1,0:T(8,128)(2,1)}, u32[]{:S(2)}, u32[]{:S(2)}) collective-permute-start(bf16[768,768]{1,0:T(8,128)(2,1)} %get-tuple-element.22), channel_id=1, source_target_pairs={{0,24},{8,16},{16,8},{24,0},{1,25},{9,17},{17,9},{25,1},{2,26},{10... | collective-permute-start | bytes 3538952 | tf_op jit(solution)/shard_map/ppermute | solution.py:215
  17.3 5.5 copy-start.5
  17.7 19.0 %copy-start = (f32[16,128,128]{1,2,0:T(8,128)}, f32[16,128,128]{1,2,0:T(8,128)S(1)}, u32[]{:S(2)}) copy-start(f32[16,128,128]{1,2,0:T(8,128)S(1)} %fusion.3) | copy-start | bytes 3145732
  37.7 24.4 %all-to-all-start.2 = ((bf16[8,64,768]{2,1,0:T(8,128)(2,1)}), bf16[8,64,768]{2,1,0:T(8,128)(2,1)}, u32[]{:S(2)}, u32[]{:S(2)}) async-start(bf16[8,64,768]{2,1,0:T(8,128)(2,1)} %broadcast_select_fusion.3), calls=%async_computation.2 | async-start | bytes 1572864 | tf_op jit(solution)/shard_map/all_to_all | solution.py:277
  62.0 57.8 %all-to-all-start.1 = ((bf16[8,160,768]{2,1,0:T(8,128)(2,1)}), bf16[8,160,768]{2,1,0:T(8,128)(2,1)}, u32[]{:S(2)}, u32[]{:S(2)}) async-start(bf16[8,160,768]{2,1,0:T(8,128)(2,1)} %bitcast.16), calls=%async_computation.1 | async-start | bytes 3932160 | tf_op jit(solution)/shard_map/all_to_all | solution.py:277
  66.8 401.7 %all-gather.15.cloned.1.call-start = ((), (), s32[]{:S(2)}) async-start(), calls=%async_computation.11 | async-start | bytes 3932160 | tf_op jit(solution)/shard_map/all_gather | solution.py:294
  66.9 27.7 %collective-permute-start = (bf16[768,768]{1,0:T(8,128)(2,1)S(1)}, bf16[768,768]{1,0:T(8,128)(2,1)}, u32[]{:S(2)}, u32[]{:S(2)}) collective-permute-start(bf16[768,768]{1,0:T(8,128)(2,1)S(1)} %get-tuple-element.25.refs_0_), channel_id=1, source_target_pairs={{0,8},{8,0},{16,24},{24,16},{1,9},{9,1},{17,25},{25,17},{2,10},{10... | collective-permute-start | bytes 3538952 | tf_op jit(solution)/shard_map/ppermute | solution.py:216
  67.0 52.8 %collective-permute-start.3 = (bf16[768,768]{1,0:T(8,128)(2,1)}, bf16[768,768]{1,0:T(8,128)(2,1)}, u32[]{:S(2)}, u32[]{:S(2)}) collective-permute-start(bf16[768,768]{1,0:T(8,128)(2,1)} %get-tuple-element.23.refs_4_), channel_id=1, source_target_pairs={{0,8},{8,0},{16,24},{24,16},{1,9},{9,1},{17,25},{25,17},{2,10},{10... | collective-permute-start | bytes 3538952 | tf_op jit(solution)/shard_map/ppermute | solution.py:216
  68.4 76.6 %collective-permute-start.2 = (bf16[768,768]{1,0:T(8,128)(2,1)}, bf16[768,768]{1,0:T(8,128)(2,1)}, u32[]{:S(2)}, u32[]{:S(2)}) collective-permute-start(bf16[768,768]{1,0:T(8,128)(2,1)} %collective-permute-done.1.refs_2_), channel_id=1, source_target_pairs={{0,8},{8,0},{16,24},{24,16},{1,9},{9,1},{17,25},{25,17},{2,10},{10... | collective-permute-start | bytes 3538952 | tf_op jit(solution)/shard_map/ppermute | solution.py:217
  68.6 101.8 %collective-permute-start.5 = (bf16[768,768]{1,0:T(8,128)(2,1)}, bf16[768,768]{1,0:T(8,128)(2,1)}, u32[]{:S(2)}, u32[]{:S(2)}) collective-permute-start(bf16[768,768]{1,0:T(8,128)(2,1)} %collective-permute-done.4.refs_6_), channel_id=1, source_target_pairs={{0,8},{8,0},{16,24},{24,16},{1,9},{9,1},{17,25},{25,17},{2,10},{10... | collective-permute-start | bytes 3538952 | tf_op jit(solution)/shard_map/ppermute | solution.py:217
  198.5 316.6 %all-gather.13.cloned.1.call-start = ((), (), s32[]{:S(2)}) async-start(), calls=%async_computation.10 | async-start | bytes 9830400 | tf_op jit(solution)/shard_map/all_gather | solution.py:294
  248.6 299.1 %all-gather.11.cloned.1.call-start = ((), (), s32[]{:S(2)}) async-start(), calls=%async_computation.9 | async-start | bytes 15728640 | tf_op jit(solution)/shard_map/all_gather | solution.py:294
  383.7 0.7 copy-start.11
  383.7 0.7 copy-start.12
  383.7 1.8 copy-start.1
  383.7 1.8 copy-start.6
  385.7 6.0 copy-start.7
  385.7 7.5 %copy-start.8 = (f32[16384,1]{0,1:T(1,128)S(1)}, f32[16384,1]{0,1:T(1,128)}, u32[]{:S(2)}) copy-start(f32[16384,1]{0,1:T(1,128)} %param.11) | copy-start | bytes 196612
  385.7 11.1 %copy-start.9 = (s32[4]{0:T(128)S(1)}, s32[4]{0:T(128)}, u32[]{:S(2)}) copy-start(s32[4]{0:T(128)} %constant.184.clone) | copy-start | bytes 52
  385.8 11.1 %copy-start.10 = (s32[4]{0:T(128)S(1)}, s32[4]{0:T(128)}, u32[]{:S(2)}) copy-start(s32[4]{0:T(128)} %constant.189) | copy-start | bytes 52
  385.8 29.6 %all-to-all-start.4 = ((bf16[8,160,768]{2,1,0:T(8,128)(2,1)}), bf16[8,160,768]{2,1,0:T(8,128)(2,1)S(1)}, u32[]{:S(2)}, u32[]{:S(2)}) async-start(bf16[8,160,768]{2,1,0:T(8,128)(2,1)} %bitcast.22), calls=%async_computation.4 | async-start | bytes 3932160 | tf_op jit(solution)/shard_map/all_to_all | solution.py:277
  390.5 203.4 %all-gather.9.cloned.1.call-start = ((), (), s32[]{:S(2)}) async-start(), calls=%async_computation.8 | async-start | bytes 9830400 | tf_op jit(solution)/shard_map/all_gather | solution.py:294
  415.4 1.3 copy-start.3
Sparse Core Ops, SparseCore 0:
  198.7 36.6 all-gather.14
  248.7 75.7 all-gather.12
  383.9 115.7 all-gather.10
  501.1 77.1 all-gather.8
